TPU v7x, 32 devices: a whole 2x2x4 slice. The times are simulated.
32 devices in a mesh: row: 4 (over y, x), col: 8 (over z, core).
Axes of the slice: x: 2, y: 2, z: 4, core: 2. Of those that a mesh axis runs over, the one named last changes fastest.
Arguments:
- x_iterate: float32 [2048, 2048], P('row', 'col'), may hold values from -6 to 6
- z_inverse: float32 [2048, 2048], P('row', 'col'), may hold values from -0.25 to 0.25
- edge_src: int32 [8, 8, 64], P('row', 'col'), may hold values from 0 to 255
- edge_dst: int32 [8, 8, 64], P('row', 'col'), may hold values from 0 to 255
- edge_count: int32 [8, 8], P('row', 'col'), may hold values from 1 to 64, as said below
Outputs:
- schur_row: float32 [8, 8, 64], P('row', 'col')
Inputs may be any that keep to these rules, and one draw needn't show every extreme that they name: `edge_count`: slots at and beyond a block pair's count are ignored; some block pair has all 64 slots live in every draw.
All inputs are finite; a program needn't handle non-finite values.
Results may differ from a plain program's by a relative error of at most 0.0001.
Values sent between devices are 32-bit elements; how exact they have to be, the bound alone decides.
No kernel may reach another device: no remote copies, remote signals or barrier semaphores. Data moves between devices by JAX's collectives and lax.ppermute only.
A program may use at most 64 MiB of HBM per device.

v0:
```python
import jax
import jax.numpy as jnp
from jax import lax
from jax.sharding import PartitionSpec as P


def from_behind(shard, axis, by):
    peers = lax.axis_size(axis)
    return lax.ppermute(shard, axis, [(i, (i + by) % peers) for i in range(peers)])


def body(x_iterate, z_inverse, edge_src, edge_dst, edge_count):
    width = x_iterate.shape[1]
    cells = x_iterate.shape[0] // width
    n_col = lax.axis_size("col")
    levels = n_col.bit_length() - 1
    row_index = lax.axis_index("row")
    col_index = lax.axis_index("col")
    grid_rows = row_index * cells + jnp.arange(cells, dtype=jnp.int32)
    slots = edge_src.shape[2]
    rows_at = edge_src.reshape(cells, slots)
    cols_at = edge_dst.reshape(cells, slots)
    x_cells = x_iterate.reshape(cells, width, width)
    z_cells = z_inverse.reshape(cells, width, width)

    def accumulate(total, left, right):
        return total + jnp.einsum("aij,ajk->aik", left, right, precision=lax.Precision.HIGHEST)

    total = jnp.zeros((cells, width, width), jnp.float32)
    for level in range(levels):
        moved = from_behind(x_cells, "col", -(1 << level))
        taken = grid_rows >> level & 1 == 1
        x_cells = jnp.where(taken[:, None, None], moved, x_cells)
    for level in range(levels):
        stride = 1 << level
        if stride % cells == 0:
            moved = from_behind(z_cells, "row", -(stride // cells))
        else:
            incoming = from_behind(z_cells[:stride], "row", -1)
            moved = jnp.concatenate([z_cells[stride:], incoming], axis=0)
        z_cells = jnp.where(col_index >> level & 1 == 1, moved, z_cells)
    total = accumulate(total, x_cells, z_cells)
    x_cells = from_behind(x_cells, "col", -1)
    incoming = from_behind(z_cells[:1], "row", -1)
    z_cells = jnp.concatenate([z_cells[1:], incoming], axis=0)
    total = accumulate(total, x_cells, z_cells)
    flat = total.reshape(cells, width * width)
    values = jnp.take_along_axis(flat, rows_at * width + cols_at, axis=1)
    live = jnp.arange(slots, dtype=jnp.int32)[None, :] < edge_count
    result = jnp.where(live, values, jnp.zeros_like(values))
    return result.reshape(cells, 1, slots)


def solution(mesh):
    return jax.shard_map(
        body,
        mesh=mesh,
        in_specs=(
            P("row", "col"),
            P("row", "col"),
            P("row", "col", None),
            P("row", "col", None),
            P("row", "col"),
        ),
        out_specs=P("row", "col", None),
        check_vma=False,
    )
```

profile of v0, /device:TPU:0, one launch (start us, length us, event | category | flops | bytes accessed | tf_op | source)
XLA Modules:
  0.0 64.5 jit_solution(1133666958314192236)
XLA Ops:
  0.0 0.0 copy-start.1
  0.0 4.5 %collective-permute-start = (f32[2,256,256]{2,1,0:T(8,128)}, f32[2,256,256]{2,1,0:T(8,128)S(1)}, u32[]{:S(2)}, u32[]{:S(2)}) collective-permute-start(f32[2,256,256]{2,1,0:T(8,128)} %bitcast.23), channel_id=1, source_target_pairs={{0,7},{1,0},{2,1},{3,2},{4,3},{5,4},{6,5},{7,6},{8,15},{9,8},{10,9... | collective-permute-start | bytes 1572872 | tf_op jit(solution)/shard_map/ppermute | solution.py:9
  4.5 1.1 %slice_bitcast_fusion.1 = (f32[1,256,256]{2,1,0:T(8,128)S(1)}, f32[1,256,256]{2,1,0:T(8,128)S(1)}) fusion(f32[512,256]{1,0:T(8,128)} %param.6), kind=kLoop, calls=%fused_computation.9 | loop fusion | bytes 1048576 | tf_op jit(solution)/shard_map/slice | solution.py:40
  5.6 2.5 %collective-permute-start.3 = (f32[1,256,256]{2,1,0:T(8,128)S(1)}, f32[1,256,256]{2,1,0:T(8,128)S(1)}, u32[]{:S(2)}, u32[]{:S(2)}) collective-permute-start(f32[1,256,256]{2,1,0:T(8,128)S(1)} %get-tuple-element.8), channel_id=1, source_target_pairs={{0,24},{8,0},{16,8},{24,16},{1,25},{9,1},{17,9},{25,17},{2,26},{10... | collective-permute-start | bytes 786440 | tf_op jit(solution)/shard_map/ppermute | solution.py:9
  8.1 0.0 copy-start
  8.1 3.4 %collective-permute-done = f32[2,256,256]{2,1,0:T(8,128)S(1)} collective-permute-done((f32[2,256,256]{2,1,0:T(8,128)}, f32[2,256,256]{2,1,0:T(8,128)S(1)}, u32[]{:S(2)}, u32[]{:S(2)}) %collective-permute-start) | collective-permute-done | bytes 524320 | tf_op jit(solution)/shard_map/ppermute | solution.py:9
  11.5 0.0 copy-done.1
  11.5 0.1 broadcast_select_fusion
  11.7 0.7 %collective-permute-start.1 = (f32[2,256,256]{2,1,0:T(8,128)S(1)}, f32[2,256,256]{2,1,0:T(8,128)S(1)}, u32[]{:S(2)}, u32[]{:S(2)}) collective-permute-start(f32[2,256,256]{2,1,0:T(8,128)S(1)} %broadcast_select_fusion), channel_id=1, source_target_pairs={{0,6},{1,7},{2,0},{3,1},{4,2},{5,3},{6,4},{7,5},{8,14},{9,15},{10,... | collective-permute-start | bytes 1572872 | tf_op jit(solution)/shard_map/ppermute | solution.py:9
  12.4 0.0 collective-permute-done.3
  12.4 0.0 copy-done
  12.4 0.9 %maximum_select_fusion = f32[2,256,256]{2,1,0:T(8,128)} fusion(f32[2,256,256]{2,1,0:T(8,128)S(1)} %bitcast.21, f32[1,256,256]{2,1,0:T(8,128)S(1)} %collective-permute-done.3, f32[1,256,256]{2,1,0:T(8,128)S(1)} %get-tuple-element.7, pred[]{:T(512)S(6)} %eq.35), kind=kLoop, calls=%fused_computation.3 | loop fusion | flops 262144 | bytes 1572865 | tf_op jit(solution)/shard_map/jit(_where)/select_n | solution.py:41
  13.2 3.0 %collective-permute-start.4 = (f32[2,256,256]{2,1,0:T(8,128)}, f32[2,256,256]{2,1,0:T(8,128)}, u32[]{:S(2)}, u32[]{:S(2)}) collective-permute-start(f32[2,256,256]{2,1,0:T(8,128)} %maximum_select_fusion), channel_id=1, source_target_pairs={{0,24},{8,0},{16,8},{24,16},{1,25},{9,1},{17,9},{25,17},{2,26},{10... | collective-permute-start | bytes 1572872 | tf_op jit(solution)/shard_map/ppermute | solution.py:9
  16.2 8.4 %collective-permute-done.1 = f32[2,256,256]{2,1,0:T(8,128)S(1)} collective-permute-done((f32[2,256,256]{2,1,0:T(8,128)S(1)}, f32[2,256,256]{2,1,0:T(8,128)S(1)}, u32[]{:S(2)}, u32[]{:S(2)}) %collective-permute-start.1) | collective-permute-done | bytes 524320 | tf_op jit(solution)/shard_map/ppermute | solution.py:9
  24.6 0.1 broadcast_select_fusion.1
  24.8 0.1 collective-permute-start.2
  24.8 2.5 %collective-permute-done.4 = f32[2,256,256]{2,1,0:T(8,128)} collective-permute-done((f32[2,256,256]{2,1,0:T(8,128)}, f32[2,256,256]{2,1,0:T(8,128)}, u32[]{:S(2)}, u32[]{:S(2)}) %collective-permute-start.4) | collective-permute-done | bytes 524320 | tf_op jit(solution)/shard_map/ppermute | solution.py:9
  27.3 0.1 broadcast_select_fusion.3
  27.4 0.6 collective-permute-start.5
  28.0 22.8 %collective-permute-done.2 = f32[2,256,256]{2,1,0:T(8,128)S(1)} collective-permute-done((f32[2,256,256]{2,1,0:T(8,128)S(1)}, f32[2,256,256]{2,1,0:T(8,128)S(1)}, u32[]{:S(2)}, u32[]{:S(2)}) %collective-permute-start.2) | collective-permute-done | bytes 524320 | tf_op jit(solution)/shard_map/ppermute | solution.py:9
  50.8 0.1 broadcast_select_fusion.2
  50.9 1.6 %collective-permute-start.6 = (f32[2,256,256]{2,1,0:T(8,128)S(1)}, f32[2,256,256]{2,1,0:T(8,128)S(1)}, u32[]{:S(2)}, u32[]{:S(2)}) collective-permute-start(f32[2,256,256]{2,1,0:T(8,128)S(1)} %broadcast_select_fusion.2), channel_id=1, source_target_pairs={{0,7},{1,0},{2,1},{3,2},{4,3},{5,4},{6,5},{7,6},{8,15},{9,8},{10,9... | collective-permute-start | bytes 1572872 | tf_op jit(solution)/shard_map/ppermute | solution.py:9
  52.5 0.0 collective-permute-done.5
  52.5 0.1 broadcast_select_fusion.4
  52.5 0.0 copy-start.3
  52.6 2.5 %collective-permute-start.7 = (f32[1,256,256]{2,1,0:T(8,128)S(1)}, f32[1,256,256]{2,1,0:T(8,128)S(1)}, u32[]{:S(2)}, u32[]{:S(2)}) collective-permute-start(f32[1,256,256]{2,1,0:T(8,128)S(1)} %get-tuple-element.6), channel_id=1, source_target_pairs={{0,24},{8,0},{16,8},{24,16},{1,25},{9,1},{17,9},{25,17},{2,26},{10... | collective-permute-start | bytes 786440 | tf_op jit(solution)/shard_map/ppermute | solution.py:9
  55.1 0.0 copy-start.2
  55.1 0.0 copy-done.3
  55.1 0.7 %copy-done.2 = s32[2,1,64]{2,1,0:T(1,128)S(1)} copy-done((s32[2,1,64]{2,1,0:T(1,128)S(1)}, s32[2,1,64]{2,1,0:T(1,128)}, u32[]{:S(2)}) %copy-start.2) | copy-done | bytes 536
  55.8 0.1 reshape.110
  55.9 4.0 %collective-permute-done.7 = f32[1,256,256]{2,1,0:T(8,128)S(1)} collective-permute-done((f32[1,256,256]{2,1,0:T(8,128)S(1)}, f32[1,256,256]{2,1,0:T(8,128)S(1)}, u32[]{:S(2)}, u32[]{:S(2)}) %collective-permute-start.7) | collective-permute-done | bytes 262176 | tf_op jit(solution)/shard_map/ppermute | solution.py:9
  59.9 0.0 collective-permute-done.6
  59.9 0.7 %fusion.1 = f32[2,256,256]{2,1,0:T(8,128)S(1)} fusion(f32[2,256,256]{2,1,0:T(8,128)S(1)} %collective-permute-done.6, f32[1,256,256]{2,1,0:T(8,128)S(1)} %collective-permute-done.7, f32[1,256,256]{2,1,0:T(8,128)S(1)} %get-tuple-element.5), kind=kOutput, calls=%fused_computation.4 | convolution fusion | flops 402784256 | bytes 1572864 | tf_op jit(solution)/shard_map/aij,ajk->aik/dot_general | solution.py:27
  60.5 0.7 %fusion = f32[1,2,256,256]{3,2,1,0:T(8,128)S(1)} fusion(f32[2,256,256]{2,1,0:T(8,128)S(1)} %fusion.1, f32[2,256,256]{2,1,0:T(8,128)S(1)} %broadcast_select_fusion.2, f32[2,256,256]{2,1,0:T(8,128)S(1)} %broadcast_select_fusion.4), kind=kOutput, calls=%fused_computation.2 | convolution fusion | flops 402784256 | bytes 2097152 | tf_op jit(solution)/shard_map/aij,ajk->aik/dot_general | solution.py:27
  61.2 0.4 copy.12
  61.6 1.6 %gather_fusion = f32[128]{0:T(128)S(1)} fusion(f32[2,65536]{1,0:T(2,128)S(1)} %bitcast.20, s32[128]{0:T(128)S(1)} %reshape.110), kind=kCustom, calls=%fused_computation | custom fusion | bytes 2048 | tf_op jit(solution)/shard_map/jit(take_along_axis)/gather | solution.py:48
  63.2 0.1 gather.7
  63.3 0.0 copy-start.4
  63.3 0.7 %copy-done.4 = s32[2,1]{0,1:T(1,128)S(1)} copy-done((s32[2,1]{0,1:T(1,128)S(1)}, s32[2,1]{0,1:T(1,128)}, u32[]{:S(2)}) %copy-start.4) | copy-done | bytes 32
  63.9 0.6 compare_select_fusion.2
  (5 shorter events, 0.1 us)
Async XLA Ops:
  0.0 11.5 %copy-start.1 = (f32[512,256]{1,0:T(8,128)S(1)}, f32[512,256]{1,0:T(8,128)}, u32[]{:S(2)}) copy-start(f32[512,256]{1,0:T(8,128)} %param.5) | copy-start | bytes 1572868
  0.0 11.5 %collective-permute-start = (f32[2,256,256]{2,1,0:T(8,128)}, f32[2,256,256]{2,1,0:T(8,128)S(1)}, u32[]{:S(2)}, u32[]{:S(2)}) collective-permute-start(f32[2,256,256]{2,1,0:T(8,128)} %bitcast.23), channel_id=1, source_target_pairs={{0,7},{1,0},{2,1},{3,2},{4,3},{5,4},{6,5},{7,6},{8,15},{9,8},{10,9... | collective-permute-start | bytes 1572872 | tf_op jit(solution)/shard_map/ppermute | solution.py:9
  5.6 6.8 %collective-permute-start.3 = (f32[1,256,256]{2,1,0:T(8,128)S(1)}, f32[1,256,256]{2,1,0:T(8,128)S(1)}, u32[]{:S(2)}, u32[]{:S(2)}) collective-permute-start(f32[1,256,256]{2,1,0:T(8,128)S(1)} %get-tuple-element.8), channel_id=1, source_target_pairs={{0,24},{8,0},{16,8},{24,16},{1,25},{9,1},{17,9},{25,17},{2,26},{10... | collective-permute-start | bytes 786440 | tf_op jit(solution)/shard_map/ppermute | solution.py:9
  8.1 4.3 %copy-start = (f32[512,256]{1,0:T(8,128)S(1)}, f32[512,256]{1,0:T(8,128)}, u32[]{:S(2)}) copy-start(f32[512,256]{1,0:T(8,128)} %param.6) | copy-start | bytes 1572868
  11.7 13.0 %collective-permute-start.1 = (f32[2,256,256]{2,1,0:T(8,128)S(1)}, f32[2,256,256]{2,1,0:T(8,128)S(1)}, u32[]{:S(2)}, u32[]{:S(2)}) collective-permute-start(f32[2,256,256]{2,1,0:T(8,128)S(1)} %broadcast_select_fusion), channel_id=1, source_target_pairs={{0,6},{1,7},{2,0},{3,1},{4,2},{5,3},{6,4},{7,5},{8,14},{9,15},{10,... | collective-permute-start | bytes 1572872 | tf_op jit(solution)/shard_map/ppermute | solution.py:9
  13.2 14.1 %collective-permute-start.4 = (f32[2,256,256]{2,1,0:T(8,128)}, f32[2,256,256]{2,1,0:T(8,128)}, u32[]{:S(2)}, u32[]{:S(2)}) collective-permute-start(f32[2,256,256]{2,1,0:T(8,128)} %maximum_select_fusion), channel_id=1, source_target_pairs={{0,24},{8,0},{16,8},{24,16},{1,25},{9,1},{17,9},{25,17},{2,26},{10... | collective-permute-start | bytes 1572872 | tf_op jit(solution)/shard_map/ppermute | solution.py:9
  24.8 26.0 %collective-permute-start.2 = (f32[2,256,256]{2,1,0:T(8,128)S(1)}, f32[2,256,256]{2,1,0:T(8,128)S(1)}, u32[]{:S(2)}, u32[]{:S(2)}) collective-permute-start(f32[2,256,256]{2,1,0:T(8,128)S(1)} %broadcast_select_fusion.1), channel_id=1, source_target_pairs={{0,4},{1,5},{2,6},{3,7},{4,0},{5,1},{6,2},{7,3},{8,12},{9,13},{10,... | collective-permute-start | bytes 1572872 | tf_op jit(solution)/shard_map/ppermute | solution.py:9
  27.4 25.1 %collective-permute-start.5 = (f32[2,256,256]{2,1,0:T(8,128)S(1)}, f32[2,256,256]{2,1,0:T(8,128)}, u32[]{:S(2)}, u32[]{:S(2)}) collective-permute-start(f32[2,256,256]{2,1,0:T(8,128)S(1)} %broadcast_select_fusion.3), channel_id=1, source_target_pairs={{0,16},{8,24},{16,0},{24,8},{1,17},{9,25},{17,1},{25,9},{2,18},{10... | collective-permute-start | bytes 1572872 | tf_op jit(solution)/shard_map/ppermute | solution.py:9
  50.9 9.0 %collective-permute-start.6 = (f32[2,256,256]{2,1,0:T(8,128)S(1)}, f32[2,256,256]{2,1,0:T(8,128)S(1)}, u32[]{:S(2)}, u32[]{:S(2)}) collective-permute-start(f32[2,256,256]{2,1,0:T(8,128)S(1)} %broadcast_select_fusion.2), channel_id=1, source_target_pairs={{0,7},{1,0},{2,1},{3,2},{4,3},{5,4},{6,5},{7,6},{8,15},{9,8},{10,9... | collective-permute-start | bytes 1572872 | tf_op jit(solution)/shard_map/ppermute | solution.py:9
  52.5 2.6 %copy-start.3 = (s32[2,1,64]{2,1,0:T(1,128)S(1)}, s32[2,1,64]{2,1,0:T(1,128)}, u32[]{:S(2)}) copy-start(s32[2,1,64]{2,1,0:T(1,128)} %param.7) | copy-start | bytes 1540
  52.6 7.3 %collective-permute-start.7 = (f32[1,256,256]{2,1,0:T(8,128)S(1)}, f32[1,256,256]{2,1,0:T(8,128)S(1)}, u32[]{:S(2)}, u32[]{:S(2)}) collective-permute-start(f32[1,256,256]{2,1,0:T(8,128)S(1)} %get-tuple-element.6), channel_id=1, source_target_pairs={{0,24},{8,0},{16,8},{24,16},{1,25},{9,1},{17,9},{25,17},{2,26},{10... | collective-permute-start | bytes 786440 | tf_op jit(solution)/shard_map/ppermute | solution.py:9
  55.1 0.7 %copy-start.2 = (s32[2,1,64]{2,1,0:T(1,128)S(1)}, s32[2,1,64]{2,1,0:T(1,128)}, u32[]{:S(2)}) copy-start(s32[2,1,64]{2,1,0:T(1,128)} %param.8) | copy-start | bytes 1540
  63.3 0.7 %copy-start.4 = (s32[2,1]{0,1:T(1,128)S(1)}, s32[2,1]{0,1:T(1,128)}, u32[]{:S(2)}) copy-start(s32[2,1]{0,1:T(1,128)} %param.9) | copy-start | bytes 28
where the time goes:
time: 64.8 us; the launch traced here: 64.5 us
  waiting for transfers between devices  41.1 us (63%)
  starting transfers between devices  15.4 us (24%)
  local copies, waits for them, and re-layouts  4.57 us (7%)
  other arithmetic  2.06 us (3%)
  matrix products  1.32 us (2%)
    ppermute x8, waiting for transfers between devices, from_behind(): lax.ppermute(shard, axis, [(i, (i + by) % peers) for i in range(peers)])  41.1 us
    ppermute x8, starting transfers between devices, from_behind(): lax.ppermute(shard, axis, [(i, (i + by) % peers) for i in range(peers)])  15.4 us
    unnamed x11, local copies, waits for them, and re-layouts  1.75 us
    gather x3, local copies, waits for them, and re-layouts, body(): values = jnp.take_along_axis(flat, rows_at * width + cols_at, axis=1)  1.71 us
    dot_general x2, matrix products, accumulate(): jnp.einsum('aij,ajk->aik', left, right, precision=lax.Precision.HIGHEST)  1.32 us
  transfers between devices with their start and end apart: 8, of which 5 were waited for; matrix products, arithmetic and copies ran while one was open for 4% of the time, Pallas kernels for 0%

commit v1 on v0

v1 whole, which is shorter than its diff:
```python
import functools

import jax
import jax.numpy as jnp
from jax import lax
from jax.experimental import pallas as pl
from jax.experimental.pallas import tpu as pltpu
from jax.sharding import PartitionSpec as P

AXES = ("row", "col")


def send(shard, dest):
    n_row, n_col = lax.axis_size("row"), lax.axis_size("col")
    pairs = []
    for r in range(n_row):
        for c in range(n_col):
            to_r, to_c = dest(r, c)
            pairs.append((r * n_col + c, to_r % n_row * n_col + to_c % n_col))
    return lax.ppermute(shard, AXES, pairs)


def pieces(value):
    high = value.astype(jnp.bfloat16)
    rest = value - high.astype(jnp.float32)
    middle = rest.astype(jnp.bfloat16)
    low = (rest - middle.astype(jnp.float32)).astype(jnp.bfloat16)
    return high, middle, low


def pick(index, width):
    slots = index.shape[1]
    on_diagonal = lax.broadcasted_iota(jnp.int32, (slots, slots), 0) == lax.broadcasted_iota(jnp.int32, (slots, slots), 1)
    column = jnp.sum(jnp.where(on_diagonal, jnp.broadcast_to(index, (slots, slots)), 0), axis=1, keepdims=True)
    return column == lax.broadcasted_iota(jnp.int32, (slots, width), 1)


def gather_rows_kernel(cells, width, *refs):
    index_refs, x_ref, out_refs = refs[: cells + 1], refs[cells + 1], refs[cells + 2 :]
    slots = index_refs[0].shape[2]
    for cell in range(cells):
        chosen = jnp.concatenate(
            [pick(index_refs[cell + step][cell], width) for step in range(2)], axis=0
        ).astype(jnp.float32).astype(jnp.bfloat16)
        block = x_ref[cell * width : (cell + 1) * width, :]
        rows = sum(
            jnp.dot(chosen, piece, preferred_element_type=jnp.float32) for piece in pieces(block)
        )
        out_refs[cell][0:slots, :] = rows[:slots]
        at = out_refs[cell + 1].shape[0] - slots
        out_refs[cell + 1][at:, :] = rows[slots:]


def finish_kernel(cells, width, *refs):
    x_refs = refs[: cells + 1]
    whole_ref, part_ref, dst_ref, count_ref, out_ref = refs[cells + 1 :]
    part = part_ref.shape[0]
    first = lax.axis_index("col") % cells
    late = (first * 2 + 1 >= cells).astype(jnp.int32)
    slots = dst_ref.shape[2]
    totals = [jnp.zeros((slots, width), jnp.float32) for _ in range(cells)]
    for shift in range(cells + 1):
        held = [cell for cell in (shift, shift - 1) if 0 <= cell < cells]
        at = first + shift
        wrapped = (at >= cells).astype(jnp.int32)
        at = at - cells * wrapped
        at_part = jnp.clip(at - late * (cells - part), 0, part - 1)
        block = jnp.where(wrapped == late, whole_ref[at], part_ref[at_part])
        chosen = jnp.concatenate([pick(dst_ref[cell], width) for cell in held], axis=0).astype(jnp.float32).astype(jnp.bfloat16)
        columns = sum(
            lax.dot_general(chosen, piece, (((1,), (1,)), ((), ())), preferred_element_type=jnp.float32)
            for piece in pieces(block)
        )
        terms = columns * x_refs[shift][...]
        for place, cell in enumerate(held):
            totals[cell] = totals[cell] + terms[place * slots : (place + 1) * slots]
    on_diagonal = lax.broadcasted_iota(jnp.int32, (slots, slots), 0) == lax.broadcasted_iota(jnp.int32, (slots, slots), 1)
    slot = lax.broadcasted_iota(jnp.int32, (1, slots), 1)
    for cell in range(cells):
        values = jnp.sum(totals[cell], axis=1, keepdims=True)
        line = jnp.sum(jnp.where(on_diagonal, jnp.broadcast_to(values, (slots, slots)), 0.0), axis=0, keepdims=True)
        out_ref[cell] = jnp.where(slot < count_ref[cell], line, 0.0)


def body(x_iterate, z_inverse, edge_src, edge_dst, edge_count):
    width = x_iterate.shape[1]
    cells = x_iterate.shape[0] // width
    slots = edge_src.shape[2]
    vmem = pl.BlockSpec(memory_space=pltpu.VMEM)
    z_cells = z_inverse.reshape(cells, width, width)
    indices = [send(edge_src, lambda r, c, d=d: (r, c + cells * r + d)) for d in range(cells + 1)]
    part = (cells + 1) // 2
    late = lax.axis_index("col") % cells * 2 + 1 >= cells
    z_some = jnp.where(late, z_cells[cells - part :], z_cells[:part])

    def beyond(c):
        return (c % cells * 2 + 1 >= cells) * 1

    z_whole = send(z_inverse, lambda r, c: (r - c // cells - beyond(c), c))
    z_part = send(z_some, lambda r, c: (r - c // cells - 1 + beyond(c), c))
    sizes = [slots * sum(0 <= cell < cells for cell in (d, d - 1)) for d in range(cells + 1)]
    rows = pl.pallas_call(
        functools.partial(gather_rows_kernel, cells, width),
        out_shape=[jax.ShapeDtypeStruct((size, width), jnp.float32) for size in sizes],
        in_specs=[vmem] * (cells + 2),
        out_specs=[vmem] * (cells + 1),
        compiler_params=pltpu.CompilerParams(vmem_limit_bytes=8 * 2**20),
        name="gather_rows",
    )(*indices, x_iterate)
    x_moved = [send(rows[d], lambda r, c, d=d: (r, c - cells * r - d)) for d in range(cells + 1)]
    return pl.pallas_call(
        functools.partial(finish_kernel, cells, width),
        out_shape=jax.ShapeDtypeStruct((cells, 1, slots), jnp.float32),
        in_specs=[vmem] * (cells + 5),
        out_specs=vmem,
        compiler_params=pltpu.CompilerParams(vmem_limit_bytes=8 * 2**20),
        name="finish",
    )(*x_moved, z_whole.reshape(z_cells.shape), z_part, edge_dst, edge_count.reshape(cells, 1, 1))


def solution(mesh):
    return jax.shard_map(
        body,
        mesh=mesh,
        in_specs=(
            P("row", "col"),
            P("row", "col"),
            P("row", "col", None),
            P("row", "col", None),
            P("row", "col"),
        ),
        out_specs=P("row", "col", None),
        check_vma=False,
    )
```

time: 64.8 us -> 32.4 us (0.50)
  the two profiles are of different devices: /device:TPU:0 before, /device:TPU:4 now
where the time goes in v1:
time: 32.4 us; the launch traced here: 32.1 us
  starting transfers between devices  23.8 us (73%)
  waiting for transfers between devices  5.47 us (17%)
  Pallas kernels  1.54 us (5%)
  other arithmetic  1.07 us (3%)
    ppermute x8, starting transfers between devices, send(): return lax.ppermute(shard, AXES, pairs)  23.8 us
    ppermute x8, waiting for transfers between devices, send(): return lax.ppermute(shard, AXES, pairs)  5.47 us
    pallas_call x1, Pallas kernels, body(): pl.pallas_call(functools.partial(finish_kernel, cells, width), out_shape=...  1.19 us
    select_n x1, other arithmetic, body(): z_some = jnp.where(late, z_cells[cells - part:], z_cells[:part])  1.07 us
  transfers between devices with their start and end apart: 8, of which 3 were waited for; matrix products, arithmetic and copies ran while one was open for 4% of the time, Pallas kernels for 1%

profile of v1, /device:TPU:4, one launch (start us, length us, event | category | flops | bytes accessed | tf_op | source)
XLA Modules:
  0.0 32.1 jit_solution(15631932386018361406)
XLA Ops:
  0.0 0.0 copy-start
  0.0 1.8 %collective-permute-start.6 = (f32[512,256]{1,0:T(8,128)}, f32[512,256]{1,0:T(8,128)S(1)}, u32[]{:S(2)}, u32[]{:S(2)}) collective-permute-start(f32[512,256]{1,0:T(8,128)} %param.6), channel_id=1, source_target_pairs={{0,0},{1,25},{2,26},{3,19},{4,20},{5,13},{6,14},{7,7},{8,8},{9,1},... | collective-permute-start | bytes 1572872 | tf_op jit(solution)/shard_map/ppermute | solution.py:20
  1.8 0.0 copy-start.2
  1.8 1.1 %select_bitcast_fusion = f32[1,256,256]{2,1,0:T(8,128)S(1)} fusion(f32[512,256]{1,0:T(8,128)} %param.6, pred[]{:T(512)S(6)} %ge.3), kind=kLoop, calls=%fused_computation | loop fusion | flops 65536 | bytes 786433 | tf_op jit(solution)/shard_map/jit(_where)/select_n | solution.py:94
  2.9 3.3 %collective-permute-start.7 = (f32[1,256,256]{2,1,0:T(8,128)S(1)}, f32[1,256,256]{2,1,0:T(8,128)S(1)}, u32[]{:S(2)}, u32[]{:S(2)}) collective-permute-start(f32[1,256,256]{2,1,0:T(8,128)S(1)} %select_bitcast_fusion), channel_id=1, source_target_pairs={{0,24},{1,1},{2,18},{3,27},{4,12},{5,21},{6,6},{7,15},{8,0},{9,9},... | collective-permute-start | bytes 786440 | tf_op jit(solution)/shard_map/ppermute | solution.py:20
  6.3 0.0 copy-done.2
  6.3 5.3 %collective-permute-start = (s32[2,1,64]{2,1,0:T(1,128)S(1)}, s32[2,1,64]{2,1,0:T(1,128)S(1)}, u32[]{:S(2)}, u32[]{:S(2)}) collective-permute-start(s32[2,1,64]{2,1,0:T(1,128)S(1)} %copy-done.2), channel_id=1, source_target_pairs={{0,0},{1,1},{2,2},{3,3},{4,4},{5,5},{6,6},{7,7},{8,10},{9,11},{10,... | collective-permute-start | bytes 1544 | tf_op jit(solution)/shard_map/ppermute | solution.py:20
  11.6 0.1 collective-permute-start.1
  11.6 4.2 %collective-permute-start.2 = (s32[2,1,64]{2,1,0:T(1,128)S(1)}, s32[2,1,64]{2,1,0:T(1,128)S(1)}, u32[]{:S(2)}, u32[]{:S(2)}) collective-permute-start(s32[2,1,64]{2,1,0:T(1,128)S(1)} %copy-done.2), channel_id=1, source_target_pairs={{0,2},{1,3},{2,4},{3,5},{4,6},{5,7},{6,0},{7,1},{8,12},{9,13},{10,... | collective-permute-start | bytes 1544 | tf_op jit(solution)/shard_map/ppermute | solution.py:20
  15.8 0.0 collective-permute-done.refs_0_
  15.9 0.0 collective-permute-done.1.refs_1_
  15.9 1.3 %collective-permute-done.2.refs_2_ = s32[2,1,64]{2,1,0:T(1,128)S(1)} collective-permute-done((s32[2,1,64]{2,1,0:T(1,128)S(1)}, s32[2,1,64]{2,1,0:T(1,128)S(1)}, u32[]{:S(2)}, u32[]{:S(2)}) %collective-permute-start.2) | collective-permute-done | bytes 544 | tf_op jit(solution)/shard_map/ppermute | solution.py:20
  17.1 0.0 copy-done
  17.1 0.3 %gather_rows.1 = (f32[64,256]{1,0:T(8,128)S(1)}, f32[128,256]{1,0:T(8,128)S(1)}, f32[64,256]{1,0:T(8,128)S(1)}) custom-call(s32[2,1,64]{2,1,0:T(1,128)S(1)} %collective-permute-done.refs_0_, s32[2,1,64]{2,1,0:T(1,128)S(1)} %collective-permute-done.1.refs_1_, s32[2,1,64]{2,1,0:T(1,128)S(1)} %collective-permute-done.2.refs_2_, f32[512,256]{1,0:T(8,128)S(1)} %copy-done), custom_call_target="tpu_custom_call" | custom-call | tf_op jit(solution)/shard_map/gather_rows/pallas_call | solution.py:102
  17.5 0.9 %collective-permute-start.4 = (f32[128,256]{1,0:T(8,128)S(1)}, f32[128,256]{1,0:T(8,128)S(1)}, u32[]{:S(2)}, u32[]{:S(2)}) collective-permute-start(f32[128,256]{1,0:T(8,128)S(1)} %get-tuple-element.9), channel_id=1, source_target_pairs={{0,7},{1,0},{2,1},{3,2},{4,3},{5,4},{6,5},{7,6},{8,13},{9,14},{10,... | collective-permute-start | bytes 393224 | tf_op jit(solution)/shard_map/ppermute | solution.py:20
  18.4 4.5 %collective-permute-start.3 = (f32[64,256]{1,0:T(8,128)S(1)}, f32[64,256]{1,0:T(8,128)S(1)}, u32[]{:S(2)}, u32[]{:S(2)}) collective-permute-start(f32[64,256]{1,0:T(8,128)S(1)} %get-tuple-element.8), channel_id=1, source_target_pairs={{0,0},{1,1},{2,2},{3,3},{4,4},{5,5},{6,6},{7,7},{8,14},{9,15},{10,... | collective-permute-start | bytes 196616 | tf_op jit(solution)/shard_map/ppermute | solution.py:20
  22.9 0.0 copy-start.3
  22.9 3.6 %collective-permute-start.5 = (f32[64,256]{1,0:T(8,128)S(1)}, f32[64,256]{1,0:T(8,128)S(1)}, u32[]{:S(2)}, u32[]{:S(2)}) collective-permute-start(f32[64,256]{1,0:T(8,128)S(1)} %get-tuple-element.10), channel_id=1, source_target_pairs={{0,6},{1,7},{2,0},{3,1},{4,2},{5,3},{6,4},{7,5},{8,12},{9,13},{10,... | collective-permute-start | bytes 196616 | tf_op jit(solution)/shard_map/ppermute | solution.py:20
  26.6 0.0 copy-done.3
  26.6 0.1 copy.6.refs_6_
  26.7 0.0 copy-start.1
  26.7 1.3 %collective-permute-done.3.refs_0_ = f32[64,256]{1,0:T(8,128)S(1)} collective-permute-done((f32[64,256]{1,0:T(8,128)S(1)}, f32[64,256]{1,0:T(8,128)S(1)}, u32[]{:S(2)}, u32[]{:S(2)}) %collective-permute-start.3) | collective-permute-done | bytes 65568 | tf_op jit(solution)/shard_map/ppermute | solution.py:20
  28.0 2.9 %collective-permute-done.5.refs_2_ = f32[64,256]{1,0:T(8,128)S(1)} collective-permute-done((f32[64,256]{1,0:T(8,128)S(1)}, f32[64,256]{1,0:T(8,128)S(1)}, u32[]{:S(2)}, u32[]{:S(2)}) %collective-permute-start.5) | collective-permute-done | bytes 65568 | tf_op jit(solution)/shard_map/ppermute | solution.py:20
  30.9 0.0 collective-permute-done.4.refs_1_
  30.9 0.0 collective-permute-done.7.refs_4_
  30.9 0.0 collective-permute-done.6
  30.9 0.0 copy-done.1
  30.9 1.2 %finish.1 = f32[2,1,64]{2,1,0:T(1,128)} custom-call(f32[64,256]{1,0:T(8,128)S(1)} %collective-permute-done.3.refs_0_, f32[128,256]{1,0:T(8,128)S(1)} %collective-permute-done.4.refs_1_, f32[64,256]{1,0:T(8,128)S(1)} %collective-permute-done.5.refs_2_, f32[2,256,256]{2,1,0:T(8,128)S(1)} %bitcast.4, f32[1,256,256]{2,1,0:T(8,128)S(1)} %collective-permute-done.7.refs_4_, ...), custom_call_target="tpu_custom_call" | custom-call | tf_op jit(solution)/shard_map/finish/pallas_call | solution.py:111
Async XLA Ops:
  0.0 17.1 %copy-start = (f32[512,256]{1,0:T(8,128)S(1)}, f32[512,256]{1,0:T(8,128)}, u32[]{:S(2)}) copy-start(f32[512,256]{1,0:T(8,128)} %refs_3_.1) | copy-start | bytes 1572868
  0.0 30.9 %collective-permute-start.6 = (f32[512,256]{1,0:T(8,128)}, f32[512,256]{1,0:T(8,128)S(1)}, u32[]{:S(2)}, u32[]{:S(2)}) collective-permute-start(f32[512,256]{1,0:T(8,128)} %param.6), channel_id=1, source_target_pairs={{0,0},{1,25},{2,26},{3,19},{4,20},{5,13},{6,14},{7,7},{8,8},{9,1},... | collective-permute-start | bytes 1572872 | tf_op jit(solution)/shard_map/ppermute | solution.py:20
  1.8 4.4 %copy-start.2 = (s32[2,1,64]{2,1,0:T(1,128)S(1)}, s32[2,1,64]{2,1,0:T(1,128)}, u32[]{:S(2)}) copy-start(s32[2,1,64]{2,1,0:T(1,128)} %param.7) | copy-start | bytes 1540
  2.9 28.0 %collective-permute-start.7 = (f32[1,256,256]{2,1,0:T(8,128)S(1)}, f32[1,256,256]{2,1,0:T(8,128)S(1)}, u32[]{:S(2)}, u32[]{:S(2)}) collective-permute-start(f32[1,256,256]{2,1,0:T(8,128)S(1)} %select_bitcast_fusion), channel_id=1, source_target_pairs={{0,24},{1,1},{2,18},{3,27},{4,12},{5,21},{6,6},{7,15},{8,0},{9,9},... | collective-permute-start | bytes 786440 | tf_op jit(solution)/shard_map/ppermute | solution.py:20
  6.3 9.6 %collective-permute-start = (s32[2,1,64]{2,1,0:T(1,128)S(1)}, s32[2,1,64]{2,1,0:T(1,128)S(1)}, u32[]{:S(2)}, u32[]{:S(2)}) collective-permute-start(s32[2,1,64]{2,1,0:T(1,128)S(1)} %copy-done.2), channel_id=1, source_target_pairs={{0,0},{1,1},{2,2},{3,3},{4,4},{5,5},{6,6},{7,7},{8,10},{9,11},{10,... | collective-permute-start | bytes 1544 | tf_op jit(solution)/shard_map/ppermute | solution.py:20
  11.6 4.3 %collective-permute-start.1 = (s32[2,1,64]{2,1,0:T(1,128)S(1)}, s32[2,1,64]{2,1,0:T(1,128)S(1)}, u32[]{:S(2)}, u32[]{:S(2)}) collective-permute-start(s32[2,1,64]{2,1,0:T(1,128)S(1)} %copy-done.2), channel_id=1, source_target_pairs={{0,1},{1,2},{2,3},{3,4},{4,5},{5,6},{6,7},{7,0},{8,11},{9,12},{10,... | collective-permute-start | bytes 1544 | tf_op jit(solution)/shard_map/ppermute | solution.py:20
  11.6 5.5 %collective-permute-start.2 = (s32[2,1,64]{2,1,0:T(1,128)S(1)}, s32[2,1,64]{2,1,0:T(1,128)S(1)}, u32[]{:S(2)}, u32[]{:S(2)}) collective-permute-start(s32[2,1,64]{2,1,0:T(1,128)S(1)} %copy-done.2), channel_id=1, source_target_pairs={{0,2},{1,3},{2,4},{3,5},{4,6},{5,7},{6,0},{7,1},{8,12},{9,13},{10,... | collective-permute-start | bytes 1544 | tf_op jit(solution)/shard_map/ppermute | solution.py:20
  17.5 13.4 %collective-permute-start.4 = (f32[128,256]{1,0:T(8,128)S(1)}, f32[128,256]{1,0:T(8,128)S(1)}, u32[]{:S(2)}, u32[]{:S(2)}) collective-permute-start(f32[128,256]{1,0:T(8,128)S(1)} %get-tuple-element.9), channel_id=1, source_target_pairs={{0,7},{1,0},{2,1},{3,2},{4,3},{5,4},{6,5},{7,6},{8,13},{9,14},{10,... | collective-permute-start | bytes 393224 | tf_op jit(solution)/shard_map/ppermute | solution.py:20
  18.4 9.6 %collective-permute-start.3 = (f32[64,256]{1,0:T(8,128)S(1)}, f32[64,256]{1,0:T(8,128)S(1)}, u32[]{:S(2)}, u32[]{:S(2)}) collective-permute-start(f32[64,256]{1,0:T(8,128)S(1)} %get-tuple-element.8), channel_id=1, source_target_pairs={{0,0},{1,1},{2,2},{3,3},{4,4},{5,5},{6,6},{7,7},{8,14},{9,15},{10,... | collective-permute-start | bytes 196616 | tf_op jit(solution)/shard_map/ppermute | solution.py:20
  22.9 3.7 %copy-start.3 = (s32[2,1]{0,1:T(1,128)S(1)}, s32[2,1]{0,1:T(1,128)}, u32[]{:S(2)}) copy-start(s32[2,1]{0,1:T(1,128)} %param.9) | copy-start | bytes 28
  22.9 8.0 %collective-permute-start.5 = (f32[64,256]{1,0:T(8,128)S(1)}, f32[64,256]{1,0:T(8,128)S(1)}, u32[]{:S(2)}, u32[]{:S(2)}) collective-permute-start(f32[64,256]{1,0:T(8,128)S(1)} %get-tuple-element.10), channel_id=1, source_target_pairs={{0,6},{1,7},{2,0},{3,1},{4,2},{5,3},{6,4},{7,5},{8,12},{9,13},{10,... | collective-permute-start | bytes 196616 | tf_op jit(solution)/shard_map/ppermute | solution.py:20
  26.7 4.2 %copy-start.1 = (s32[2,1,64]{2,1,0:T(1,128)S(1)}, s32[2,1,64]{2,1,0:T(1,128)}, u32[]{:S(2)}) copy-start(s32[2,1,64]{2,1,0:T(1,128)} %refs_5_.1) | copy-start | bytes 1540

commit v2 on v0

v2 whole, which is shorter than its diff:
```python
import functools

import jax
import jax.numpy as jnp
from jax import lax
from jax.experimental import pallas as pl
from jax.experimental.pallas import tpu as pltpu
from jax.sharding import PartitionSpec as P


AXES = ("row", "col")
VMEM = pl.BlockSpec(memory_space=pltpu.VMEM)
PARAMS = pltpu.CompilerParams(vmem_limit_bytes=8 * 2**20)

TERMS = tuple(
    tuple((a, b, s) for a in range(2) for b in range(2) for s in range(2) if (a + b + s) // 2 == side)
    for side in range(2)
)


def send(shard, dest):
    n_row, n_col = lax.axis_size("row"), lax.axis_size("col")
    pairs = []
    for r in range(n_row):
        for c in range(n_col):
            to_r, to_pair, to_side = dest(r, c // 2, c % 2)
            to_c = to_pair * 2 + to_side
            pairs.append((r * n_col + c, to_r % n_row * n_col + to_c % n_col))
    return lax.ppermute(shard, AXES, pairs)


def swap(shard):
    return send(shard, lambda r, pair, side: (r, pair, 1 - side))


def pieces(value):
    high = value.astype(jnp.bfloat16)
    rest = value - high.astype(jnp.float32)
    middle = rest.astype(jnp.bfloat16)
    low = (rest - middle.astype(jnp.float32)).astype(jnp.bfloat16)
    return high, middle, low


def diagonal(slots):
    return lax.broadcasted_iota(jnp.int32, (slots, slots), 0) == lax.broadcasted_iota(jnp.int32, (slots, slots), 1)


def pick(lines, width):
    columns = []
    for line in lines:
        slots = line.shape[1]
        spread = jnp.where(diagonal(slots), jnp.broadcast_to(line, (slots, slots)), 0)
        columns.append(jnp.sum(spread, axis=1, keepdims=True))
    column = jnp.concatenate(columns, axis=0)
    chosen = column == lax.broadcasted_iota(jnp.int32, (column.shape[0], width), 1)
    return chosen.astype(jnp.float32).astype(jnp.bfloat16)


def by_side(action):
    here = lax.axis_index("col") % 2
    for side in range(2):
        pl.when(here == side)(functools.partial(action, side))


def gather(side, block_of, index_ref, refs, out_ref, contract):
    slots = index_ref.shape[2]
    blocks = {}
    for place, (a, b, s) in enumerate(TERMS[side]):
        blocks.setdefault(block_of(a, b, a + b + s - 2 * side), []).append((place, a, b))
    for (which, at), wanted in blocks.items():
        width = out_ref.shape[1]
        chosen = pick([index_ref[(b ^ side) * 2 + a] for _, a, b in wanted], width)
        block = refs[which][at * width : (at + 1) * width, :]
        taken = sum(
            lax.dot_general(chosen, piece, (((1,), (contract,)), ((), ())), preferred_element_type=jnp.float32)
            for piece in pieces(block)
        )
        for n, (place, _, _) in enumerate(wanted):
            out_ref[place * slots : (place + 1) * slots, :] = taken[n * slots : (n + 1) * slots]


def gather_x_kernel(index_ref, own_ref, partner_ref, out_ref):
    @by_side
    def _(side):
        gather(side, lambda a, b, g: (g ^ side, a), index_ref, (own_ref, partner_ref), out_ref, 0)


def gather_z_kernel(index_ref, own_ref, partner_ref, out_ref):
    @by_side
    def _(side):
        def block_of(a, b, g):
            return (0, g) if b == side else (1, 0)

        gather(side, block_of, index_ref, (own_ref, partner_ref), out_ref, 1)


def dots_kernel(x_ref, z_ref, own_ref, other_ref):
    slots = own_ref.shape[2]

    def line(values):
        spread = jnp.where(diagonal(slots), jnp.broadcast_to(values, (slots, slots)), 0.0)
        return jnp.sum(spread, axis=0, keepdims=True)

    @by_side
    def _(side):
        products = [x_ref[n * slots : (n + 1) * slots, :] * z_ref[n * slots : (n + 1) * slots, :] for n in range(len(TERMS[side]))]
        for b in range(2):
            for a in range(2):
                mine = [products[n] for n, term in enumerate(TERMS[side]) if term[:2] == (a, b)]
                if mine:
                    out = line(jnp.sum(sum(mine[1:], mine[0]), axis=1, keepdims=True))
                    if b == side:
                        own_ref[a] = out
                    else:
                        other_ref[0] = out


def finish_kernel(own_ref, other_ref, count_ref, out_ref):
    slots = out_ref.shape[2]
    slot = lax.broadcasted_iota(jnp.int32, (1, slots), 1)
    shared = 1 - lax.axis_index("col") % 2
    for a in range(2):
        value = own_ref[a] + jnp.where(shared == a, other_ref[0], 0.0)
        out_ref[a] = jnp.where(slot < count_ref[a], value, 0.0)


def call(kernel, shapes, *operands):
    return pl.pallas_call(
        kernel,
        out_shape=[jax.ShapeDtypeStruct(shape, jnp.float32) for shape in shapes],
        in_specs=[VMEM] * len(operands),
        out_specs=[VMEM] * len(shapes),
        compiler_params=PARAMS,
    )(*operands)


def body(x_iterate, z_inverse, edge_src, edge_dst, edge_count):
    width = x_iterate.shape[1]
    slots = edge_src.shape[2]
    assert x_iterate.shape[0] == 2 * width
    side = lax.axis_index("col") % 2
    src_partner = swap(edge_src)
    dst_partner = swap(edge_dst)
    x_partner = swap(x_iterate)
    z_partner = swap(lax.dynamic_slice_in_dim(z_inverse, side * width, width, axis=0))
    src = jnp.concatenate([edge_src, src_partner], axis=0)
    dst = jnp.concatenate([edge_dst, dst_partner], axis=0)
    src = send(src, lambda r, pair, side: (r, pair + r + side, side))
    dst = send(dst, lambda r, pair, side: (r + pair + side, pair, side))
    terms = [(len(TERMS[0]) * slots, width)]
    (rows,) = call(gather_x_kernel, terms, src, x_iterate, x_partner)
    rows = send(rows, lambda r, pair, side: (r, pair - r - side, side))
    (columns,) = call(gather_z_kernel, terms, dst, z_inverse, z_partner)
    columns = send(columns, lambda r, pair, side: (r - pair - side, pair, side))
    own, other = call(dots_kernel, [(2, 1, slots), (1, 1, slots)], rows, columns)
    other = swap(other)
    (out,) = call(finish_kernel, [(2, 1, slots)], own, other, edge_count.reshape(2, 1, 1))
    return out


def solution(mesh):
    return jax.shard_map(
        body,
        mesh=mesh,
        in_specs=(
            P("row", "col"),
            P("row", "col"),
            P("row", "col", None),
            P("row", "col", None),
            P("row", "col"),
        ),
        out_specs=P("row", "col", None),
        check_vma=False,
    )
```

time: 64.8 us -> 29.2 us (0.45)
  the two profiles are of different devices: /device:TPU:0 before, /device:TPU:5 now
where the time goes in v2:
time: 29.2 us; the launch traced here: 29 us
  starting transfers between devices  16.9 us (58%)
  waiting for transfers between devices  8.93 us (31%)
  Pallas kernels  1.91 us (7%)
  local copies, waits for them, and re-layouts  1.11 us (4%)
    ppermute x9, starting transfers between devices, send(): return lax.ppermute(shard, AXES, pairs)  16.9 us
    ppermute x9, waiting for transfers between devices, send(): return lax.ppermute(shard, AXES, pairs)  8.93 us
    pallas_call x4, Pallas kernels, call(): pl.pallas_call(kernel, out_shape=[jax.ShapeDtypeStruct(shape, jnp.float32...  1.91 us
    dynamic_slice x1, local copies, waits for them, and re-layouts, body(): lax.dynamic_slice_in_dim(z_inverse, side * width, width, axis=0)  0.99 us
  transfers between devices with their start and end apart: 9, of which 3 were waited for; matrix products, arithmetic and copies ran while one was open for 4% of the time, Pallas kernels for 4%

profile of v2, /device:TPU:5, one launch (start us, length us, event | category | flops | bytes accessed | tf_op | source)
XLA Modules:
  0.0 29.0 jit_solution(15735723659926602741)
XLA Ops:
  0.0 0.0 copy-start
  0.0 0.7 %collective-permute-start.2 = (f32[512,256]{1,0:T(8,128)}, f32[512,256]{1,0:T(8,128)S(1)}, u32[]{:S(2)}, u32[]{:S(2)}) collective-permute-start(f32[512,256]{1,0:T(8,128)} %own_ref.2), channel_id=1, source_target_pairs={{0,1},{1,0},{2,3},{3,2},{4,5},{5,4},{6,7},{7,6},{8,9},{9,8},{10,11... | collective-permute-start | bytes 1572872 | tf_op jit(solution)/shard_map/ppermute | solution.py:29
  0.7 0.0 copy-start.2
  0.7 0.0 copy-start.3
  0.7 1.0 %constant_dynamic-slice_fusion = f32[256,256]{1,0:T(8,128)S(1)} fusion(f32[512,256]{1,0:T(8,128)} %own_ref.3, s32[]{:T(128)S(6)} %select_n.11), kind=kLoop, calls=%fused_computation.2 | loop fusion | bytes 524292 | tf_op jit(solution)/shard_map/dynamic_slice | solution.py:145
  1.7 0.1 collective-permute-start.6
  1.8 0.0 copy-done.2
  1.8 0.5 %collective-permute-start.4 = (s32[2,1,64]{2,1,0:T(1,128)S(1)}, s32[2,1,64]{2,1,0:T(1,128)S(1)}, u32[]{:S(2)}, u32[]{:S(2)}) collective-permute-start(s32[2,1,64]{2,1,0:T(1,128)S(1)} %copy-done.2), channel_id=1, source_target_pairs={{0,1},{1,0},{2,3},{3,2},{4,5},{5,4},{6,7},{7,6},{8,9},{9,8},{10,11... | collective-permute-start | bytes 1544 | tf_op jit(solution)/shard_map/ppermute | solution.py:29
  2.3 0.0 copy-done.3
  2.3 0.1 collective-permute-start
  2.3 0.9 %collective-permute-done.4 = s32[2,1,64]{2,1,0:T(1,128)S(1)} collective-permute-done((s32[2,1,64]{2,1,0:T(1,128)S(1)}, s32[2,1,64]{2,1,0:T(1,128)S(1)}, u32[]{:S(2)}, u32[]{:S(2)}) %collective-permute-start.4) | collective-permute-done | bytes 544 | tf_op jit(solution)/shard_map/ppermute | solution.py:29
  3.3 3.1 %collective-permute-start.5 = (s32[4,1,64]{2,1,0:T(1,128)S(1)}, s32[4,1,64]{2,1,0:T(1,128)S(1)}, u32[]{:S(2)}, u32[]{:S(2)}) collective-permute-start(s32[4,1,64]{2,1,0:T(1,128)S(1)} %pad_add_fusion.1), channel_id=1, source_target_pairs={{0,0},{1,9},{2,10},{3,19},{4,20},{5,29},{6,30},{7,7},{8,8},{9,17},... | collective-permute-start | bytes 3080 | tf_op jit(solution)/shard_map/ppermute | solution.py:29
  6.4 0.0 collective-permute-done
  6.4 0.0 copy-start.1
  6.4 2.9 %collective-permute-start.1 = (s32[4,1,64]{2,1,0:T(1,128)S(1)}, s32[4,1,64]{2,1,0:T(1,128)S(1)}, u32[]{:S(2)}, u32[]{:S(2)}) collective-permute-start(s32[4,1,64]{2,1,0:T(1,128)S(1)} %pad_add_fusion), channel_id=1, source_target_pairs={{0,0},{1,3},{2,2},{3,5},{4,4},{5,7},{6,6},{7,1},{8,10},{9,13},{10,... | collective-permute-start | bytes 3080 | tf_op jit(solution)/shard_map/ppermute | solution.py:29
  9.4 0.0 collective-permute-done.5.index_ref
  9.4 0.0 collective-permute-done.6.partner_ref
  9.4 0.0 copy-done
  9.4 0.6 %shard_map.56 = f32[256,256]{1,0:T(8,128)S(1)} custom-call(s32[4,1,64]{2,1,0:T(1,128)S(1)} %collective-permute-done.5.index_ref, f32[512,256]{1,0:T(8,128)S(1)} %copy-done, f32[256,256]{1,0:T(8,128)S(1)} %collective-permute-done.6.partner_ref), custom_call_target="tpu_custom_call" | custom-call | tf_op jit(solution)/shard_map/pallas_call | solution.py:128
  10.0 3.6 %collective-permute-start.7 = (f32[256,256]{1,0:T(8,128)S(1)}, f32[256,256]{1,0:T(8,128)S(1)}, u32[]{:S(2)}, u32[]{:S(2)}) collective-permute-start(f32[256,256]{1,0:T(8,128)S(1)} %shard_map.56), channel_id=1, source_target_pairs={{0,0},{1,25},{2,26},{3,19},{4,20},{5,13},{6,14},{7,7},{8,8},{9,1},... | collective-permute-start | bytes 786440 | tf_op jit(solution)/shard_map/ppermute | solution.py:29
  13.6 0.0 collective-permute-done.1.index_ref
  13.6 0.0 collective-permute-done.2.partner_ref
  13.6 0.0 copy-done.1
  13.6 0.5 %shard_map.55 = f32[256,256]{1,0:T(8,128)S(1)} custom-call(s32[4,1,64]{2,1,0:T(1,128)S(1)} %collective-permute-done.1.index_ref, f32[512,256]{1,0:T(8,128)S(1)} %copy-done.1, f32[512,256]{1,0:T(8,128)S(1)} %collective-permute-done.2.partner_ref), custom_call_target="tpu_custom_call" | custom-call | tf_op jit(solution)/shard_map/pallas_call | solution.py:128
  14.1 3.2 %collective-permute-start.3 = (f32[256,256]{1,0:T(8,128)S(1)}, f32[256,256]{1,0:T(8,128)S(1)}, u32[]{:S(2)}, u32[]{:S(2)}) collective-permute-start(f32[256,256]{1,0:T(8,128)S(1)} %shard_map.55), channel_id=1, source_target_pairs={{0,0},{1,7},{2,2},{3,1},{4,4},{5,3},{6,6},{7,5},{8,14},{9,13},{10,... | collective-permute-start | bytes 786440 | tf_op jit(solution)/shard_map/ppermute | solution.py:29
  17.3 0.0 collective-permute-done.7.z_ref
  17.3 7.3 %collective-permute-done.3.x_ref = f32[256,256]{1,0:T(8,128)S(1)} collective-permute-done((f32[256,256]{1,0:T(8,128)S(1)}, f32[256,256]{1,0:T(8,128)S(1)}, u32[]{:S(2)}, u32[]{:S(2)}) %collective-permute-start.3) | collective-permute-done | bytes 262176 | tf_op jit(solution)/shard_map/ppermute | solution.py:29
  24.6 0.1 shard_map.57
  24.7 0.0 copy-start.4
  24.7 2.8 %collective-permute-start.8 = (f32[1,1,64]{2,1,0:T(1,128)S(1)}, f32[1,1,64]{2,1,0:T(1,128)S(1)}, u32[]{:S(2)}, u32[]{:S(2)}) collective-permute-start(f32[1,1,64]{2,1,0:T(1,128)S(1)} %get-tuple-element.8), channel_id=1, source_target_pairs={{0,1},{1,0},{2,3},{3,2},{4,5},{5,4},{6,7},{7,6},{8,9},{9,8},{10,11... | collective-permute-start | bytes 776 | tf_op jit(solution)/shard_map/ppermute | solution.py:29
  27.5 0.0 copy-done.4
  27.5 0.1 copy.6.count_ref
  27.6 0.7 %collective-permute-done.8.other_ref = f32[1,1,64]{2,1,0:T(1,128)S(1)} collective-permute-done((f32[1,1,64]{2,1,0:T(1,128)S(1)}, f32[1,1,64]{2,1,0:T(1,128)S(1)}, u32[]{:S(2)}, u32[]{:S(2)}) %collective-permute-start.8) | collective-permute-done | bytes 288 | tf_op jit(solution)/shard_map/ppermute | solution.py:29
  28.3 0.6 %shard_map.58 = f32[2,1,64]{2,1,0:T(1,128)} custom-call(f32[2,1,64]{2,1,0:T(1,128)S(1)} %get-tuple-element.7.own_ref, f32[1,1,64]{2,1,0:T(1,128)S(1)} %collective-permute-done.8.other_ref, s32[2,1,1]{2,1,0:T(1,128)S(1)} %copy.6.count_ref), custom_call_target="tpu_custom_call" | custom-call | tf_op jit(solution)/shard_map/pallas_call | solution.py:128
  (2 shorter events, 0.0 us)
Async XLA Ops:
  0.0 9.4 %copy-start = (f32[512,256]{1,0:T(8,128)S(1)}, f32[512,256]{1,0:T(8,128)}, u32[]{:S(2)}) copy-start(f32[512,256]{1,0:T(8,128)} %own_ref.3) | copy-start | bytes 1572868
  0.0 13.6 %collective-permute-start.2 = (f32[512,256]{1,0:T(8,128)}, f32[512,256]{1,0:T(8,128)S(1)}, u32[]{:S(2)}, u32[]{:S(2)}) collective-permute-start(f32[512,256]{1,0:T(8,128)} %own_ref.2), channel_id=1, source_target_pairs={{0,1},{1,0},{2,3},{3,2},{4,5},{5,4},{6,7},{7,6},{8,9},{9,8},{10,11... | collective-permute-start | bytes 1572872 | tf_op jit(solution)/shard_map/ppermute | solution.py:29
  0.7 1.1 %copy-start.2 = (s32[2,1,64]{2,1,0:T(1,128)S(1)}, s32[2,1,64]{2,1,0:T(1,128)}, u32[]{:S(2)}) copy-start(s32[2,1,64]{2,1,0:T(1,128)} %param.8) | copy-start | bytes 1540
  0.7 1.6 %copy-start.3 = (s32[2,1,64]{2,1,0:T(1,128)S(1)}, s32[2,1,64]{2,1,0:T(1,128)}, u32[]{:S(2)}) copy-start(s32[2,1,64]{2,1,0:T(1,128)} %param.7) | copy-start | bytes 1540
  1.7 7.7 %collective-permute-start.6 = (f32[256,256]{1,0:T(8,128)S(1)}, f32[256,256]{1,0:T(8,128)S(1)}, u32[]{:S(2)}, u32[]{:S(2)}) collective-permute-start(f32[256,256]{1,0:T(8,128)S(1)} %constant_dynamic-slice_fusion), channel_id=1, source_target_pairs={{0,1},{1,0},{2,3},{3,2},{4,5},{5,4},{6,7},{7,6},{8,9},{9,8},{10,11... | collective-permute-start | bytes 786440 | tf_op jit(solution)/shard_map/ppermute | solution.py:29
  1.8 1.5 %collective-permute-start.4 = (s32[2,1,64]{2,1,0:T(1,128)S(1)}, s32[2,1,64]{2,1,0:T(1,128)S(1)}, u32[]{:S(2)}, u32[]{:S(2)}) collective-permute-start(s32[2,1,64]{2,1,0:T(1,128)S(1)} %copy-done.2), channel_id=1, source_target_pairs={{0,1},{1,0},{2,3},{3,2},{4,5},{5,4},{6,7},{7,6},{8,9},{9,8},{10,11... | collective-permute-start | bytes 1544 | tf_op jit(solution)/shard_map/ppermute | solution.py:29
  2.3 4.1 %collective-permute-start = (s32[2,1,64]{2,1,0:T(1,128)S(1)}, s32[2,1,64]{2,1,0:T(1,128)S(1)}, u32[]{:S(2)}, u32[]{:S(2)}) collective-permute-start(s32[2,1,64]{2,1,0:T(1,128)S(1)} %copy-done.3), channel_id=1, source_target_pairs={{0,1},{1,0},{2,3},{3,2},{4,5},{5,4},{6,7},{7,6},{8,9},{9,8},{10,11... | collective-permute-start | bytes 1544 | tf_op jit(solution)/shard_map/ppermute | solution.py:29
  3.3 6.1 %collective-permute-start.5 = (s32[4,1,64]{2,1,0:T(1,128)S(1)}, s32[4,1,64]{2,1,0:T(1,128)S(1)}, u32[]{:S(2)}, u32[]{:S(2)}) collective-permute-start(s32[4,1,64]{2,1,0:T(1,128)S(1)} %pad_add_fusion.1), channel_id=1, source_target_pairs={{0,0},{1,9},{2,10},{3,19},{4,20},{5,29},{6,30},{7,7},{8,8},{9,17},... | collective-permute-start | bytes 3080 | tf_op jit(solution)/shard_map/ppermute | solution.py:29
  6.4 7.2 %copy-start.1 = (f32[512,256]{1,0:T(8,128)S(1)}, f32[512,256]{1,0:T(8,128)}, u32[]{:S(2)}) copy-start(f32[512,256]{1,0:T(8,128)} %own_ref.2) | copy-start | bytes 1572868
  6.4 7.2 %collective-permute-start.1 = (s32[4,1,64]{2,1,0:T(1,128)S(1)}, s32[4,1,64]{2,1,0:T(1,128)S(1)}, u32[]{:S(2)}, u32[]{:S(2)}) collective-permute-start(s32[4,1,64]{2,1,0:T(1,128)S(1)} %pad_add_fusion), channel_id=1, source_target_pairs={{0,0},{1,3},{2,2},{3,5},{4,4},{5,7},{6,6},{7,1},{8,10},{9,13},{10,... | collective-permute-start | bytes 3080 | tf_op jit(solution)/shard_map/ppermute | solution.py:29
  10.0 7.3 %collective-permute-start.7 = (f32[256,256]{1,0:T(8,128)S(1)}, f32[256,256]{1,0:T(8,128)S(1)}, u32[]{:S(2)}, u32[]{:S(2)}) collective-permute-start(f32[256,256]{1,0:T(8,128)S(1)} %shard_map.56), channel_id=1, source_target_pairs={{0,0},{1,25},{2,26},{3,19},{4,20},{5,13},{6,14},{7,7},{8,8},{9,1},... | collective-permute-start | bytes 786440 | tf_op jit(solution)/shard_map/ppermute | solution.py:29
  14.1 10.4 %collective-permute-start.3 = (f32[256,256]{1,0:T(8,128)S(1)}, f32[256,256]{1,0:T(8,128)S(1)}, u32[]{:S(2)}, u32[]{:S(2)}) collective-permute-start(f32[256,256]{1,0:T(8,128)S(1)} %shard_map.55), channel_id=1, source_target_pairs={{0,0},{1,7},{2,2},{3,1},{4,4},{5,3},{6,6},{7,5},{8,14},{9,13},{10,... | collective-permute-start | bytes 786440 | tf_op jit(solution)/shard_map/ppermute | solution.py:29
  24.7 2.8 %copy-start.4 = (s32[2,1]{0,1:T(1,128)S(1)}, s32[2,1]{0,1:T(1,128)}, u32[]{:S(2)}) copy-start(s32[2,1]{0,1:T(1,128)} %param.9) | copy-start | bytes 28
  24.7 3.6 %collective-permute-start.8 = (f32[1,1,64]{2,1,0:T(1,128)S(1)}, f32[1,1,64]{2,1,0:T(1,128)S(1)}, u32[]{:S(2)}, u32[]{:S(2)}) collective-permute-start(f32[1,1,64]{2,1,0:T(1,128)S(1)} %get-tuple-element.8), channel_id=1, source_target_pairs={{0,1},{1,0},{2,3},{3,2},{4,5},{5,4},{6,7},{7,6},{8,9},{9,8},{10,11... | collective-permute-start | bytes 776 | tf_op jit(solution)/shard_map/ppermute | solution.py:29
